TPU v7x, 256 devices: a whole 4x4x8 slice. The times are simulated.
256 devices in a mesh: gx: 16 (over z, core), gy: 4 (over x), gz: 4 (over y).
Axes of the slice: x: 4, y: 4, z: 8, core: 2. Of those that a mesh axis runs over, the one named last changes fastest.
Arguments:
- block_values: bfloat16 [4, 64, 4, 6, 128, 128], P('gy', 'gx', 'gz'), as said below
- block_cols: int32 [4, 64, 4, 6], P('gy', 'gx', 'gz'), may hold values from 0 to 63, as said below
Outputs:
- purified: float32 [2048, 32768], P(('gx', 'gy'), 'gz')
Inputs may be any that keep to these rules, and one draw needn't show every extreme that they name: block_cols[a, s, b, :] holds 6 distinct tile columns of panel b at which tile row a * 64 + s of P is nonzero; every tile column of a panel is listed by exactly 6 tile rows of each slab; the pattern is symmetric: tile (i, j) is listed exactly when tile (j, i) is. `block_values`: P is symmetric: the tile listed at (i, j) is the transpose of the tile listed at (j, i), and diagonal tiles are symmetric.
All inputs are finite; a program needn't handle non-finite values.
Results may differ from a plain program's by a relative error of at most 0.0033.
Values may be sent and summed in bfloat16 or wider, within the bound.
A program may use at most 128 MiB of HBM per device.

v0:
```python
import jax
import jax.numpy as jnp
from jax import lax
from jax.sharding import PartitionSpec as P

WIN = 1


def picked_2(x, axis, root):
    return lax.dynamic_index_in_dim(lax.all_gather(x, axis), root, 0, keepdims=False)


def in_blocks(x, dim, length):
    lengths = x.shape
    tiles = x.reshape(*lengths[:dim], length, lengths[dim] // length, *lengths[dim + 1 :])
    return jnp.moveaxis(tiles, dim, 0)


def sent_and_summed(x, axis, dim):
    tiles = in_blocks(x, dim, lax.axis_size(axis))
    arrived = lax.all_to_all(tiles, axis, split_axis=0, concat_axis=0, tiled=True)
    return arrived.astype(jnp.float32).sum(axis=0)


def densify(left_tiles, left_columns, slab_tiles):
    onehot = (
        left_columns[:, :, None] == jnp.arange(slab_tiles, dtype=jnp.int32)[None, None, :]
    ).astype(jnp.bfloat16)
    densified = jnp.einsum("wkj,wkyx->wyjx", onehot, left_tiles, preferred_element_type=jnp.float32)
    tile_size = left_tiles.shape[2]
    return densified.astype(jnp.bfloat16).reshape(
        left_tiles.shape[0] * tile_size, slab_tiles, tile_size
    )


def product_one(left_panel, panel_tiles, panel_columns):
    summed = jnp.zeros(
        (left_panel.shape[0], panel_tiles.shape[0], panel_tiles.shape[2]), jnp.float32
    )
    for column_slot in range(panel_tiles.shape[1]):
        picked = jnp.take(left_panel, panel_columns[:, column_slot], axis=1)
        summed = summed + jnp.einsum(
            "rix,iyx->riy", picked, panel_tiles[:, column_slot], preferred_element_type=jnp.float32
        )
    return summed


def product_two(rounded, panel_tiles, panel_columns, panel_width):
    summed = jnp.zeros((rounded.shape[0], panel_width, panel_tiles.shape[3]), jnp.float32)
    for column_slot in range(panel_tiles.shape[1]):
        product = jnp.einsum(
            "rix,ixy->riy", rounded, panel_tiles[:, column_slot], preferred_element_type=jnp.float32
        )
        summed = summed.at[:, panel_columns[:, column_slot], :].add(product)
    return summed


def local(block_values, block_cols):
    tiles_here = block_values[0, :, 0]
    columns_here = block_cols[0, :, 0]
    tile_size = tiles_here.shape[2]
    slab_tiles = tiles_here.shape[0] * lax.axis_size("gx")
    left_tiles, left_columns = (
        picked_2(tiles_here[:WIN], "gy", 0),
        picked_2(columns_here[:WIN], "gy", 0),
    )
    left_panel = densify(left_tiles, left_columns, slab_tiles)
    height = left_panel.shape[0]
    on_diagonal = (lax.axis_index("gy") == lax.axis_index("gz")).astype(jnp.float32)
    panel_tiles, panel_columns = (
        lax.all_gather(tiles_here, "gx", axis=0, tiled=True),
        lax.all_gather(columns_here, "gx", axis=0, tiled=True),
    )
    partial_square = product_one(left_panel, panel_tiles, panel_columns)
    partial_square = partial_square.reshape(height, slab_tiles * tile_size)
    square = lax.psum(partial_square, "gz")
    square_low = square.astype(jnp.bfloat16).reshape(height, slab_tiles, tile_size)
    applied = product_two(square_low, panel_tiles, panel_columns, slab_tiles).reshape(
        height // lax.axis_size("gy") * lax.axis_size("gy"), slab_tiles * tile_size
    )
    return sent_and_summed(
        (3.0 * on_diagonal * square - 2.0 * applied).astype(jnp.bfloat16), "gy", 0
    )


def solution(mesh):
    in_specs = (P("gy", "gx", "gz", None, None, None), P("gy", "gx", "gz", None))
    out_specs = P(("gx", "gy"), "gz")
    return jax.shard_map(local, mesh=mesh, in_specs=in_specs, out_specs=out_specs, check_vma=False)
```

profile of v0, /device:TPU:32, one launch (start us, length us, event | category | flops | bytes accessed | tf_op | source)
XLA Modules:
  0.0 381.8 jit_solution(5912386459244780532)
XLA Ops:
  8.8 9.7 %all-gather = s32[4,1,1,6]{3,2,1,0:T(1,128)S(1)} all-gather(s32[1,1,1,6]{3,2,1,0:T(1,128)S(1)} %slice-done.4), channel_id=2, replica_groups=mesh['gx'=16,'gy'=4,'gz'=4] {'gy'}, dimensions={0}, use_global_device_ids=true | all-gather | bytes 120 | tf_op jit(solution)/shard_map/all_gather | solution.py:10
  18.5 13.3 %all-gather.1 = bf16[4,1,1,6,128,128]{5,4,3,2,1,0:T(8,128)(2,1)S(1)} all-gather(bf16[1,1,1,6,128,128]{5,4,3,2,1,0:T(8,128)(2,1)S(1)} %slice-done.3), channel_id=3, replica_groups=mesh['gx'=16,'gy'=4,'gz'=4] {'gy'}, dimensions={0}, use_global_device_ids=true | all-gather | bytes 983040 | tf_op jit(solution)/shard_map/all_gather | solution.py:10
  34.1 18.6 %all-gather.2 = s32[1,64,1,6]{3,2,0,1:T(1,128)S(1)} all-gather(s32[1,4,1,6]{3,2,0,1:T(1,128)S(1)} %bitcast.101), channel_id=4, replica_groups=mesh['gx'=16,'gy'=4,'gz'=4] {'gx'}, dimensions={1}, use_global_device_ids=true | all-gather | bytes 1632 | tf_op jit(solution)/shard_map/all_gather | solution.py:72
  66.1 19.6 %all-gather.6.cloned.1.call-done = bf16[1,64,1,6,128,128]{5,4,1,3,2,0:T(8,128)(2,1)} async-done(((bf16[1,4,1,6,128,128]{5,4,1,3,2,0:T(8,128)(2,1)}), bf16[1,64,1,6,128,128]{5,4,1,3,2,0:T(8,128)(2,1)}) %all-gather.6.cloned.1.call-update) | async-done | bytes 12582928 | tf_op jit(solution)/shard_map/all_gather | solution.py:71
  85.7 6.2 %fusion.10 = f32[64,128,128]{1,2,0:T(8,128)} fusion(bf16[64,128,128]{2,1,0:T(8,128)(2,1)} %gather_fusion, pred[64]{0:T(512)(128)(4,1)S(1)} %get-tuple-element.29, bf16[64,6,128,128]{3,2,0,1:T(8,128)(2,1)} %bitcast.84), kind=kOutput, calls=%fused_computation.31 | convolution fusion | flops 269484032 | bytes 8388672 | tf_op jit(solution)/shard_map/rix,iyx->riy/dot_general | solution.py:42
  91.8 6.0 %fusion.2 = f32[64,128,128]{1,2,0:T(8,128)} fusion(bf16[64,128,128]{2,1,0:T(8,128)(2,1)} %gather_fusion.4, pred[64]{0:T(512)(128)(4,1)S(1)} %get-tuple-element.25, bf16[64,6,128,128]{3,2,0,1:T(8,128)(2,1)} %bitcast.85), kind=kOutput, calls=%fused_computation.23 | convolution fusion | flops 269484032 | bytes 8388672 | tf_op jit(solution)/shard_map/rix,iyx->riy/dot_general | solution.py:42
  97.8 3.6 fusion.4
  101.5 3.6 fusion.6
  105.1 3.6 fusion.8
  108.7 10.1 %add_add_fusion = f32[64,128,128]{1,2,0:T(8,128)} fusion(f32[64,128,128]{1,2,0:T(8,128)} %fusion.2, f32[64,128,128]{1,2,0:T(8,128)} %fusion.4, f32[64,128,128]{1,2,0:T(8,128)} %fusion.6, f32[64,128,128]{1,2,0:T(8,128)} %fusion.10, f32[64,128,128]{1,2,0:T(8,128)} %fusion.8, bf16[64,128,128]{2,1,0:T(8,128)(2,1)S(1)} %copy-done.4, ...), kind=kOutput, calls=%fused_computation.15 | convolution fusion | flops 274726912 | bytes 29360640 | tf_op jit(solution)/shard_map/rix,iyx->riy/dot_general | solution.py:42
  118.8 98.5 %all-reduce.2.cloned.1.call-done = f32[128,8192]{0,1:T(8,128)} async-done(((f32[128,8192]{0,1:T(8,128)}), f32[128,8192]{0,1:T(8,128)}) %all-reduce.2.cloned.1.call-update) | async-done | bytes 4194320 | tf_op jit(solution)/shard_map/psum | solution.py:76
  219.9 4.6 %fusion.24 = f32[64,128,128]{2,1,0:T(8,128)} fusion(bf16[128,64,128]{0,2,1:T(8,128)(2,1)S(1)} %bitcast.78, bf16[64,6,128,128]{3,2,0,1:T(8,128)(2,1)} %bitcast.86), kind=kOutput, calls=%fused_computation.47 | convolution fusion | flops 268435456 | bytes 8388608 | tf_op jit(solution)/shard_map/rix,ixy->riy/dot_general | solution.py:51
  224.5 4.6 %fusion.25 = f32[64,128,128]{2,1,0:T(8,128)} fusion(bf16[128,64,128]{0,2,1:T(8,128)(2,1)S(1)} %bitcast.79, bf16[64,6,128,128]{3,2,0,1:T(8,128)(2,1)} %bitcast.87), kind=kOutput, calls=%fused_computation.48 | convolution fusion | flops 268435456 | bytes 8388608 | tf_op jit(solution)/shard_map/rix,ixy->riy/dot_general | solution.py:51
  242.8 13.7 %scatter_fusion = f32[128,64,128]{2,0,1:T(8,128)} fusion(f32[128,64,128]{2,0,1:T(8,128)} %broadcast_in_dim.11, s32[64]{0:T(128)S(1)} %get-tuple-element.7, f32[64,128,128]{2,1,0:T(8,128)} %fusion.24), kind=kCustom, calls=%fused_computation.6 | custom fusion | flops 1048576 | bytes 12583168 | tf_op jit(solution)/shard_map/scatter-add | solution.py:54
  256.5 13.7 %scatter_fusion.1 = f32[128,64,128]{2,0,1:T(8,128)} fusion(f32[128,64,128]{2,0,1:T(8,128)} %scatter_fusion, s32[64]{0:T(128)S(1)} %get-tuple-element.8, f32[64,128,128]{2,1,0:T(8,128)} %fusion.25), kind=kCustom, calls=%fused_computation.7 | custom fusion | flops 1048576 | bytes 12583168 | tf_op jit(solution)/shard_map/scatter-add | solution.py:54
  270.2 13.7 %scatter_fusion.2 = f32[128,64,128]{2,0,1:T(8,128)} fusion(f32[128,64,128]{2,0,1:T(8,128)} %scatter_fusion.1, s32[64]{0:T(128)S(1)} %get-tuple-element.9, f32[64,128,128]{2,1,0:T(8,128)} %fusion.26), kind=kCustom, calls=%fused_computation.8 | custom fusion | flops 1048576 | bytes 12583168 | tf_op jit(solution)/shard_map/scatter-add | solution.py:54
  283.9 13.6 %scatter_fusion.3 = f32[128,64,128]{2,0,1:T(8,128)} fusion(f32[128,64,128]{2,0,1:T(8,128)} %scatter_fusion.2, s32[64]{0:T(128)S(1)} %get-tuple-element.10, f32[64,128,128]{2,1,0:T(8,128)} %fusion.27), kind=kCustom, calls=%fused_computation.9 | custom fusion | flops 1048576 | bytes 12583168 | tf_op jit(solution)/shard_map/scatter-add | solution.py:54
  297.5 13.7 %scatter_fusion.4 = f32[128,64,128]{2,0,1:T(8,128)} fusion(f32[128,64,128]{2,0,1:T(8,128)} %scatter_fusion.3, s32[64]{0:T(128)S(1)} %get-tuple-element.11, f32[64,128,128]{2,1,0:T(8,128)} %fusion.28), kind=kCustom, calls=%fused_computation.10 | custom fusion | flops 1048576 | bytes 12583168 | tf_op jit(solution)/shard_map/scatter-add | solution.py:54
  311.1 13.6 %scatter_fusion.5 = f32[128,64,128]{2,0,1:T(8,128)} fusion(f32[128,64,128]{2,0,1:T(8,128)} %scatter_fusion.4, s32[64]{0:T(128)S(1)} %get-tuple-element.6, f32[64,128,128]{2,1,0:T(8,128)} %fusion.29), kind=kCustom, calls=%fused_computation.11 | custom fusion | flops 1048576 | bytes 12583168 | tf_op jit(solution)/shard_map/scatter-add | solution.py:54
  324.8 4.7 %broadcast_multiply_fusion = f32[128,64,128]{2,0,1:T(8,128)} fusion(f32[128,64,128]{2,0,1:T(8,128)} %scatter_fusion.5), kind=kLoop, calls=%fused_computation.39 | loop fusion | flops 1048576 | bytes 8388608 | tf_op jit(solution)/shard_map/mul | solution.py:82
  329.5 5.6 %copy.42 = f32[128,64,128]{0,2,1:T(8,128)} copy(f32[128,64,128]{2,0,1:T(8,128)} %broadcast_multiply_fusion) | data formatting | bytes 8388608 | tf_op jit(solution)/shard_map/mul | solution.py:82
  335.1 5.2 %fusion = bf16[128,8192]{0,1:T(8,128)(2,1)} fusion(f32[128,64,128]{0,2,1:T(8,128)} %copy.42, f32[128,8192]{0,1:T(8,128)} %all-reduce.2.cloned.1.call-done, f32[]{:T(128)S(6)} %mul_shard_map.3), kind=kLoop, calls=%fused_computation.13 | loop fusion | flops 3145728 | bytes 10485764 | tf_op jit(solution)/shard_map/convert_element_type | solution.py:82
  340.3 2.9 copy.43
  343.3 30.4 %all_to_all.5 = bf16[4,32,8192]{2,1,0:T(8,128)(2,1)S(1)} all-to-all(bf16[4,32,8192]{2,1,0:T(8,128)(2,1)S(1)} %bitcast.99), channel_id=1, replica_groups=mesh['gx'=16,'gy'=4,'gz'=4] {'gy'}, dimensions={0} | all-to-all | bytes 4194304 | tf_op jit(solution)/shard_map/all_to_all | solution.py:21
  (58 shorter events, 35.4 us)
Async XLA Ops:
  6.5 12.0 %slice-start.3 = ((bf16[1,4,1,6,128,128]{5,4,3,2,1,0:T(8,128)(2,1)}), bf16[1,1,1,6,128,128]{5,4,3,2,1,0:T(8,128)(2,1)S(1)}, s32[]{:S(2)}) async-start(bf16[1,4,1,6,128,128]{5,4,3,2,1,0:T(8,128)(2,1)} %param.4), calls=%async_computation.6 | async-start | bytes 393216 | tf_op jit(solution)/shard_map/slice | solution.py:64
  6.5 2.2 slice-start.4
  6.5 79.1 %all-gather.6.cloned.1.call-start = ((), (), s32[]{:S(2)}) async-start(), calls=%async_computation.2 | async-start | bytes 13369344 | tf_op jit(solution)/shard_map/all_gather | solution.py:71
  8.7 208.6 %all-reduce.2.cloned.1.call-start = ((), (), s32[]{:S(2)}) async-start(), calls=%async_computation.1 | async-start | bytes 8388608 | tf_op jit(solution)/shard_map/psum | solution.py:76
  32.7 1.4 copy-start.5
  85.7 12.2 %copy-start = (bf16[1,64,1,6,128,128]{5,4,1,3,2,0:T(8,128)(2,1)S(1)}, bf16[1,64,1,6,128,128]{5,4,1,3,2,0:T(8,128)(2,1)}, u32[]{:S(2)}) copy-start(bf16[1,64,1,6,128,128]{5,4,1,3,2,0:T(8,128)(2,1)} %all-gather.6.cloned.1.call-done) | copy-start | bytes 37748740
  91.8 6.0 %copy-start.1 = (bf16[64,128,128]{2,1,0:T(8,128)(2,1)S(1)}, bf16[64,128,128]{2,1,0:T(8,128)(2,1)}, u32[]{:S(2)}) copy-start(bf16[64,128,128]{2,1,0:T(8,128)(2,1)} %gather_fusion.3) | copy-start | bytes 6291460
  97.8 3.6 copy-start.2
  101.5 3.6 copy-start.3
  105.1 3.6 copy-start.4
  217.4 11.7 %slice-start = ((s8[12582912]{0:T(1024)(128)(4,1)}), s8[4194304]{0:T(1024)(128)(4,1)S(1)}, s32[]{:S(2)}) async-start(s8[12582912]{0:T(1024)(128)(4,1)} %bitcast.92), calls=%async_computation.3 | async-start | bytes 8388608
  219.9 9.2 %slice-start.1 = ((s8[12582912]{0:T(1024)(128)(4,1)}), s8[4194304]{0:T(1024)(128)(4,1)S(1)}, s32[]{:S(2)}) async-start(s8[12582912]{0:T(1024)(128)(4,1)} %bitcast.92), calls=%async_computation.4 | async-start | bytes 8388608
  224.5 4.6 %slice-start.2 = ((s8[12582912]{0:T(1024)(128)(4,1)}), s8[4194304]{0:T(1024)(128)(4,1)S(1)}, s32[]{:S(2)}) async-start(s8[12582912]{0:T(1024)(128)(4,1)} %bitcast.92), calls=%async_computation.5 | async-start | bytes 8388608
Sparse Core Ops, SparseCore 0:
  9.2 76.4 all-gather.5
  118.9 98.3 all-reduce.1
where the time goes:
time: 383 us; the launch traced here: 382 us
  waiting for transfers between devices  118 us (31%)
  other arithmetic  96.3 us (25%)
  blocking collectives  72 us (19%)
  matrix products  54.3 us (14%)
  local copies, waits for them, and re-layouts  27.4 us (7%)
  between operations  13.5 us (4%)
    psum x1, waiting for transfers between devices, local(): square = lax.psum(partial_square, 'gz')  98.5 us
    scatter-add x6, other arithmetic, product_two(): summed = summed.at[:, panel_columns[:, column_slot], :].add(product)  82 us
    dot_general x6, matrix products, product_one(): jnp.einsum('rix,iyx->riy', picked, panel_tiles[:, column_slot], preferred...  33.1 us
    all_to_all x1, blocking collectives, sent_and_summed(): lax.all_to_all(tiles, axis, split_axis=0, concat_axis=0, tiled=True)  30.4 us
    all_gather x2, blocking collectives, picked_2(): lax.all_gather(x, axis)  23 us
    dot_general x6, matrix products, product_two(): jnp.einsum('rix,ixy->riy', rounded, panel_tiles[:, column_slot], preferre...  20.4 us
    all_gather x1, waiting for transfers between devices, local(): lax.all_gather(tiles_here, 'gx', axis=0, tiled=True)  19.6 us
    all_gather x1, blocking collectives, local(): lax.all_gather(columns_here, 'gx', axis=0, tiled=True)  18.6 us
  transfers between devices with their start and end apart: 2, of which 2 were waited for; matrix products, arithmetic and copies ran while one was open for 4% of the time, Pallas kernels for 0%

commit v1 on v0

--- a/solution.py
+++ b/solution.py
@@ -1,9 +1,25 @@
+import functools
 import jax
 import jax.numpy as jnp
 from jax import lax
 from jax.sharding import PartitionSpec as P
 
 WIN = 1
+
+
+def _advance_rails(inner_x, row_dim):
+    shares = lax.axis_size("gx")
+    lanes = tuple((shares if t == row_dim else 1 for t in range(inner_x.ndim)))
+    return lax.all_to_all(
+        jnp.tile(inner_x, lanes),
+        axis_name="gx",
+        split_axis=row_dim,
+        concat_axis=row_dim,
+        tiled=True,
+    )
+
+
+compute_the_sides = functools.partial(_advance_rails, row_dim=0)
 
 
 def picked_2(x, axis, root):
@@ -68,7 +84,7 @@
     height = left_panel.shape[0]
     on_diagonal = (lax.axis_index("gy") == lax.axis_index("gz")).astype(jnp.float32)
     panel_tiles, panel_columns = (
-        lax.all_gather(tiles_here, "gx", axis=0, tiled=True),
+        compute_the_sides(tiles_here),
         lax.all_gather(columns_here, "gx", axis=0, tiled=True),
     )
     partial_square = product_one(left_panel, panel_tiles, panel_columns)

time: 383 us -> 621 us (1.62)
  blocking collectives: 72 us -> 310 us
  waiting for transfers between devices: 118 us -> 99.3 us
  starting transfers between devices: 0.04 us -> 8.75 us
  local copies, waits for them, and re-layouts: 27.4 us -> 35.1 us
    all_gather x1, blocking collectives: 18.6 us -> 256 us  [local(): lax.all_gather(columns_here, 'gx', axis=0, tiled=True)]
    all_gather x1 -> x0, waiting for transfers between devices: 19.6 us -> none  [local(): lax.all_gather(tiles_here, 'gx', axis=0, tiled=True)]
    another operation x0 -> x1, local copies, waits for them, and re-layouts: none -> 8.82 us  [_advance_rails(): jnp.tile(inner_x, lanes)]
    all_to_all x0 -> x1, starting transfers between devices: none -> 8.72 us  [_advance_rails(): lax.all_to_all(jnp.tile(inner_x, lanes), axis_name='gx', split_axis=row_d...]
  transfers between devices with their start and end apart: 2 -> 2, of which waited for: 2 -> 1; matrix products, arithmetic and copies ran while one was open for 4% -> 3% of each run, Pallas kernels for 0% -> 0%
where the time goes in v1:
time: 621 us; the launch traced here: 620 us
  blocking collectives  310 us (50%)
  waiting for transfers between devices  99.3 us (16%)
  other arithmetic  96.4 us (16%)
  matrix products  56.8 us (9%)
  local copies, waits for them, and re-layouts  35.1 us (6%)
  between operations  13.6 us (2%)
  starting transfers between devices  8.75 us (1%)
    all_gather x1, blocking collectives, local(): lax.all_gather(columns_here, 'gx', axis=0, tiled=True)  256 us
    psum x1, waiting for transfers between devices, local(): square = lax.psum(partial_square, 'gz')  99.3 us
    scatter-add x6, other arithmetic, product_two(): summed = summed.at[:, panel_columns[:, column_slot], :].add(product)  82.3 us
    all_to_all x1, blocking collectives, sent_and_summed(): lax.all_to_all(tiles, axis, split_axis=0, concat_axis=0, tiled=True)  30 us
    dot_general x6, matrix products, product_one(): jnp.einsum('rix,iyx->riy', picked, panel_tiles[:, column_slot], preferred...  29.6 us
    dot_general x6, matrix products, product_two(): jnp.einsum('rix,ixy->riy', rounded, panel_tiles[:, column_slot], preferre...  26.3 us
    all_gather x2, blocking collectives, picked_2(): lax.all_gather(x, axis)  23.7 us
    gather x6, local copies, waits for them, and re-layouts, product_one(): picked = jnp.take(left_panel, panel_columns[:, column_slot], axis=1)  12.9 us
  transfers between devices with their start and end apart: 2, of which 1 were waited for; matrix products, arithmetic and copies ran while one was open for 3% of the time, Pallas kernels for 0%

profile of v1, /device:TPU:32, one launch (start us, length us, event | category | flops | bytes accessed | tf_op | source)
XLA Modules:
  0.0 619.6 jit_solution(15630794862738572767)
XLA Ops:
  6.5 8.8 %tile.11 = bf16[16,4,6,128,128]{4,3,2,1,0:T(8,128)(2,1)} broadcast(bf16[4,6,128,128]{3,2,1,0:T(8,128)(2,1)} %bitcast.101), dimensions={1,2,3,4} | broadcast | bytes 13369344 | tf_op jit(solution)/shard_map/tile | solution.py:14
  15.4 8.7 %all-to-all-start = ((bf16[64,6,128,128]{3,2,1,0:T(8,128)(2,1)}), bf16[64,6,128,128]{3,2,1,0:T(8,128)(2,1)}, u32[]{:S(2)}, u32[]{:S(2)}) async-start(bf16[64,6,128,128]{3,2,1,0:T(8,128)(2,1)} %bitcast.97), calls=%async_computation | async-start | bytes 25165824 | tf_op jit(solution)/shard_map/all_to_all | solution.py:13
  24.1 9.7 %all-gather = s32[4,1,1,6]{3,2,1,0:T(1,128)S(1)} all-gather(s32[1,1,1,6]{3,2,1,0:T(1,128)S(1)} %slice-done), channel_id=2, replica_groups=mesh['gx'=16,'gy'=4,'gz'=4] {'gy'}, dimensions={0}, use_global_device_ids=true | all-gather | bytes 120 | tf_op jit(solution)/shard_map/all_gather | solution.py:26
  34.8 13.9 %all-gather.1 = bf16[4,1,1,6,128,128]{5,4,3,2,1,0:T(8,128)(2,1)S(1)} all-gather(bf16[1,1,1,6,128,128]{5,4,3,2,1,0:T(8,128)(2,1)S(1)} %slice.59), channel_id=3, replica_groups=mesh['gx'=16,'gy'=4,'gz'=4] {'gy'}, dimensions={0}, use_global_device_ids=true | all-gather | bytes 983040 | tf_op jit(solution)/shard_map/all_gather | solution.py:26
  51.0 256.0 %all-gather.2 = s32[1,64,1,6]{3,2,0,1:T(1,128)S(1)} all-gather(s32[1,4,1,6]{3,2,0,1:T(1,128)S(1)} %bitcast.102), channel_id=4, replica_groups=mesh['gx'=16,'gy'=4,'gz'=4] {'gx'}, dimensions={1}, use_global_device_ids=true | all-gather | bytes 1632 | tf_op jit(solution)/shard_map/all_gather | solution.py:88
  331.4 5.3 fusion.6
  336.7 5.4 fusion.8
  342.0 8.1 %add_add_fusion = f32[64,128,128]{1,2,0:T(8,128)} fusion(f32[64,128,128]{1,2,0:T(8,128)S(1)} %fusion.2, f32[64,128,128]{1,2,0:T(8,128)S(1)} %fusion.4, f32[64,128,128]{1,2,0:T(8,128)} %fusion.6, f32[64,128,128]{1,2,0:T(8,128)S(1)} %fusion.10, f32[64,128,128]{1,2,0:T(8,128)} %fusion.8, bf16[64,128,128]{2,1,0:T(8,128)(2,1)S(1)} %copy-done.4, ...), kind=kOutput, calls=%fused_computation.15 | convolution fusion | flops 274726912 | bytes 29360192 | tf_op jit(solution)/shard_map/rix,iyx->riy/dot_general | solution.py:58
  350.2 99.3 %all-reduce.2.cloned.1.call-done = f32[128,8192]{0,1:T(8,128)} async-done(((f32[128,8192]{0,1:T(8,128)}), f32[128,8192]{0,1:T(8,128)}) %all-reduce.2.cloned.1.call-update) | async-done | bytes 4194320 | tf_op jit(solution)/shard_map/psum | solution.py:92
  451.9 4.4 fusion.24
  458.7 13.9 %scatter_fusion = f32[128,64,128]{2,0,1:T(8,128)} fusion(f32[128,64,128]{2,0,1:T(8,128)} %broadcast_in_dim.11, s32[64]{0:T(128)S(1)} %get-tuple-element.7, f32[64,128,128]{2,1,0:T(8,128)} %fusion.24), kind=kCustom, calls=%fused_computation.6 | custom fusion | flops 1048576 | bytes 12583168 | tf_op jit(solution)/shard_map/scatter-add | solution.py:70
  472.6 4.4 fusion.25
  477.0 13.7 %scatter_fusion.1 = f32[128,64,128]{2,0,1:T(8,128)} fusion(f32[128,64,128]{2,0,1:T(8,128)} %scatter_fusion, s32[64]{0:T(128)S(1)} %get-tuple-element.8, f32[64,128,128]{2,1,0:T(8,128)} %fusion.25), kind=kCustom, calls=%fused_computation.7 | custom fusion | flops 1048576 | bytes 12583168 | tf_op jit(solution)/shard_map/scatter-add | solution.py:70
  490.7 4.4 fusion.26
  495.1 13.7 %scatter_fusion.2 = f32[128,64,128]{2,0,1:T(8,128)} fusion(f32[128,64,128]{2,0,1:T(8,128)} %scatter_fusion.1, s32[64]{0:T(128)S(1)} %get-tuple-element.9, f32[64,128,128]{2,1,0:T(8,128)} %fusion.26), kind=kCustom, calls=%fused_computation.8 | custom fusion | flops 1048576 | bytes 12583168 | tf_op jit(solution)/shard_map/scatter-add | solution.py:70
  508.8 4.4 fusion.27
  513.2 13.6 %scatter_fusion.3 = f32[128,64,128]{2,0,1:T(8,128)} fusion(f32[128,64,128]{2,0,1:T(8,128)} %scatter_fusion.2, s32[64]{0:T(128)S(1)} %get-tuple-element.10, f32[64,128,128]{2,1,0:T(8,128)} %fusion.27), kind=kCustom, calls=%fused_computation.9 | custom fusion | flops 1048576 | bytes 12583168 | tf_op jit(solution)/shard_map/scatter-add | solution.py:70
  526.8 4.4 fusion.28
  531.2 13.8 %scatter_fusion.4 = f32[128,64,128]{2,0,1:T(8,128)} fusion(f32[128,64,128]{2,0,1:T(8,128)} %scatter_fusion.3, s32[64]{0:T(128)S(1)} %get-tuple-element.11, f32[64,128,128]{2,1,0:T(8,128)} %fusion.28), kind=kCustom, calls=%fused_computation.10 | custom fusion | flops 1048576 | bytes 12583168 | tf_op jit(solution)/shard_map/scatter-add | solution.py:70
  549.4 13.6 %scatter_fusion.5 = f32[128,64,128]{2,0,1:T(8,128)} fusion(f32[128,64,128]{2,0,1:T(8,128)} %scatter_fusion.4, s32[64]{0:T(128)S(1)} %get-tuple-element.6, f32[64,128,128]{2,1,0:T(8,128)} %fusion.29), kind=kCustom, calls=%fused_computation.11 | custom fusion | flops 1048576 | bytes 12583168 | tf_op jit(solution)/shard_map/scatter-add | solution.py:70
  563.0 4.7 broadcast_multiply_fusion
  567.7 5.6 copy.47
  573.3 5.2 fusion
  581.4 30.0 %all_to_all.10 = bf16[4,32,8192]{2,1,0:T(8,128)(2,1)S(1)} all-to-all(bf16[4,32,8192]{2,1,0:T(8,128)(2,1)S(1)} %bitcast.99), channel_id=1, replica_groups=mesh['gx'=16,'gy'=4,'gz'=4] {'gy'}, dimensions={0} | all-to-all | bytes 4194304 | tf_op jit(solution)/shard_map/all_to_all | solution.py:37
  (49 shorter events, 40.9 us)
Async XLA Ops:
  15.4 8.8 %slice-start = ((s32[1,4,1,6]{3,2,1,0:T(1,128)}), s32[1,1,1,6]{3,2,1,0:T(1,128)S(1)}, s32[]{:S(2)}) async-start(s32[1,4,1,6]{3,2,1,0:T(1,128)} %param.5), calls=%async_computation.3 | async-start | bytes 1024 | tf_op jit(solution)/shard_map/slice | solution.py:81
  15.4 305.1 %all-to-all-start = ((bf16[64,6,128,128]{3,2,1,0:T(8,128)(2,1)}), bf16[64,6,128,128]{3,2,1,0:T(8,128)(2,1)}, u32[]{:S(2)}, u32[]{:S(2)}) async-start(bf16[64,6,128,128]{3,2,1,0:T(8,128)(2,1)} %bitcast.97), calls=%async_computation | async-start | bytes 25165824 | tf_op jit(solution)/shard_map/all_to_all | solution.py:13
  24.1 425.4 %all-reduce.2.cloned.1.call-start = ((), (), s32[]{:S(2)}) async-start(), calls=%async_computation.2 | async-start | bytes 8388608 | tf_op jit(solution)/shard_map/psum | solution.py:92
  49.6 1.4 copy-start.5
  320.5 4.0 copy-start
  324.5 3.4 copy-start.1
  327.9 3.4 copy-start.2
  331.3 5.3 copy-start.3
  336.7 5.4 copy-start.4
Sparse Core Ops, SparseCore 0:
  350.3 99.1 all-reduce.1
